TPU v7x, 256 devices: a whole 4x4x8 slice. The times are simulated.
256 devices in a mesh: row: 16 (over y, x), col: 8 (over z), rep: 2 (over core).
Axes of the slice: x: 4, y: 4, z: 8, core: 2. Of those that a mesh axis runs over, the one named last changes fastest.
Arguments:
- patches: bfloat16 [2, 512, 6144], P('rep', 'col', 'row'), may hold values from -6 to 6
- cotangent: bfloat16 [2, 512, 6144], P('rep', 'col', 'row'), may hold values from -6 to 6
- w_in: bfloat16 [6144, 24576], P('row', 'col'), may hold values from -0.078125 to 0.078125
- w_out: bfloat16 [24576, 6144], P('col', 'row'), may hold values from -0.0390625 to 0.0390625
- moment_in: bfloat16 [2, 6144, 24576], P('rep', 'row', 'col'), may hold values from -2 to 2
- moment_out: bfloat16 [2, 24576, 6144], P('rep', 'col', 'row'), may hold values from -2 to 2
Outputs:
- mixed: bfloat16 [2, 512, 6144], P('rep', 'col', 'row')
- tally_in: bfloat16 [6144, 24576], P('row', 'col')
- tally_out: bfloat16 [24576, 6144], P('col', 'row')
All inputs are finite; a program needn't handle non-finite values.
Results may differ from a plain program's by a relative error of at most 0.0055.
Values may be sent and summed in bfloat16 or wider, within the bound.
A program may use at most 128 MiB of HBM per device.

v0:
```python
import math
import jax
import jax.numpy as jnp
from jax import lax
from jax.sharding import PartitionSpec as P

momentum_decay = 0.9
vote_scale = 0.3


def joined_along(blocks, dim):
    blocks = jnp.moveaxis(blocks, 0, dim)
    lengths = blocks.shape
    return blocks.reshape(*lengths[:dim], lengths[dim] * lengths[dim + 1], *lengths[dim + 2 :])


def sent_to_all(value, axis):
    copies = jnp.broadcast_to(value, (lax.axis_size(axis), *value.shape))
    return lax.all_to_all(copies, axis, split_axis=0, concat_axis=0, tiled=True)


def gather_directly(value, axis, dim):
    return joined_along(sent_to_all(value, axis), dim)


def cut_along(value, dim, peers):
    before, after = (value.shape[:dim], value.shape[dim + 1 :])
    return jnp.moveaxis(value.reshape(*before, peers, -1, *after), dim, 0)


def sum_at_owner(value, axis, dim):
    blocks = cut_along(value, dim, lax.axis_size(axis))
    arrived = lax.all_to_all(blocks, axis, split_axis=0, concat_axis=0, tiled=True)
    return arrived.sum(axis=0)


def gelu_value(pre):
    return 0.5 * pre * (1.0 + lax.erf(pre * (1.0 / math.sqrt(2.0))))


def gelu_slope(pre):
    return 0.5 * (1.0 + lax.erf(pre * (1.0 / math.sqrt(2.0)))) + pre * jnp.exp(-0.5 * pre * pre) * (
        1.0 / math.sqrt(2.0 * math.pi)
    )


def shards(patches, cotangent, w_in, w_out, moment_in, moment_out):
    inputs = gather_directly(patches[0], "col", 0)
    total_rows = inputs.shape[0]
    norm_factor = 1.0 / math.sqrt(total_rows)
    pre_whole = lax.psum(jnp.dot(inputs, w_in, preferred_element_type=jnp.float32), "row")
    hidden = gelu_value(pre_whole).astype(jnp.bfloat16)
    block = hidden
    mixed = sum_at_owner(
        jnp.dot(block, w_out, preferred_element_type=jnp.float32), "col", 0
    ).astype(jnp.bfloat16)
    grads = lax.all_gather(cotangent[0], "col", axis=0, tiled=True)
    block = grads
    back_whole = lax.psum(
        lax.dot_general(
            block, w_out, (((1,), (1,)), ((), ())), preferred_element_type=jnp.float32
        ).astype(jnp.bfloat16),
        "row",
    ).astype(jnp.float32)
    slope = (back_whole * gelu_slope(pre_whole)).astype(jnp.bfloat16)
    grad_first = (
        lax.dot_general(inputs, slope, (((0,), (0,)), ((), ())), preferred_element_type=jnp.float32)
        * norm_factor
    )
    grad_second = (
        lax.dot_general(hidden, grads, (((0,), (0,)), ((), ())), preferred_element_type=jnp.float32)
        * norm_factor
    )
    moved_first = (
        momentum_decay * moment_in[0].astype(jnp.float32) + (1.0 - momentum_decay) * grad_first
    )
    moved_second = (
        momentum_decay * moment_out[0].astype(jnp.float32) + (1.0 - momentum_decay) * grad_second
    )
    vote_first = jnp.tanh(moved_first / vote_scale).astype(jnp.bfloat16)
    vote_second = jnp.tanh(moved_second / vote_scale).astype(jnp.bfloat16)
    tally_first, tally_second = (
        lax.psum(vote_first, "rep").astype(jnp.float32),
        lax.psum(vote_second, "rep").astype(jnp.float32),
    )
    return (mixed[None], tally_first.astype(jnp.bfloat16), tally_second.astype(jnp.bfloat16))


def solution(mesh):
    in_specs = (
        P("rep", "col", "row"),
        P("rep", "col", "row"),
        P("row", "col"),
        P("col", "row"),
        P("rep", "row", "col"),
        P("rep", "col", "row"),
    )
    out_specs = (P("rep", "col", "row"), P("row", "col"), P("col", "row"))
    return jax.shard_map(shards, mesh=mesh, in_specs=in_specs, out_specs=out_specs, check_vma=False)
```

profile of v0, /device:TPU:1, one launch (start us, length us, event | category | flops | bytes accessed | tf_op | source)
XLA Modules:
  0.0 338.2 jit_solution(2649844550422343762)
XLA Ops:
  7.2 0.0 all-reduce.5.cloned.1.call-start
  7.2 1.0 broadcast_in_dim.4
  8.2 22.4 %all_to_all.10 = bf16[8,64,384]{2,1,0:T(8,128)(2,1)S(1)} all-to-all(bf16[8,64,384]{2,1,0:T(8,128)(2,1)S(1)} %broadcast_in_dim.4), channel_id=1, replica_groups=mesh['row'=16,'col'=8,'rep'=2] {'col'}, dimensions={0} | all-to-all | bytes 786432 | tf_op jit(solution)/shard_map/all_to_all | solution.py:19
  30.6 6.1 %fusion.20 = f32[512,3072]{1,0:T(8,128)} fusion(bf16[512,384]{1,0:T(8,128)(2,1)S(1)} %bitcast.36, bf16[384,3072]{1,0:T(8,128)(2,1)} %param.8), kind=kOutput, calls=%fused_computation.26 | convolution fusion | flops 1207959552 | bytes 9043968 | tf_op jit(solution)/shard_map/dot_general | solution.py:51
  36.7 0.0 all-reduce.5.cloned.1.call-update
  36.7 0.0 all-reduce.7.cloned.1.call-start
  36.8 0.7 copy-done.2
  37.5 20.5 %all-gather = bf16[1,512,384]{2,1,0:T(8,128)(2,1)S(1)} all-gather(bf16[1,64,384]{2,1,0:T(8,128)(2,1)S(1)} %copy-done.2), channel_id=2, replica_groups=mesh['row'=16,'col'=8,'rep'=2] {'col'}, dimensions={1}, use_global_device_ids=true | all-gather | bytes 442368 | tf_op jit(solution)/shard_map/all_gather | solution.py:57
  58.0 3.5 %convolution_convert_fusion = bf16[512,3072]{1,0:T(8,128)(2,1)} fusion(bf16[3072,384]{1,0:T(8,128)(2,1)S(1)} %copy-done, bf16[1,512,384]{2,1,0:T(8,128)(2,1)S(1)} %all-gather), kind=kOutput, calls=%fused_computation.17 | convolution fusion | flops 1209532416 | bytes 5898240 | tf_op jit(solution)/shard_map/dot_general | solution.py:60
  61.4 0.0 all-reduce.7.cloned.1.call-update
  61.5 0.0 all-reduce.9.cloned.1.call-start
  61.5 4.3 %copy.9 = bf16[1,384,3072]{1,2,0:T(8,128)(2,1)} copy(bf16[1,384,3072]{2,1,0:T(8,128)(2,1)} %param.10) | data formatting | bytes 4718592 | tf_op args[4]
  65.8 101.0 %all-reduce.5.cloned.1.call-done = f32[512,3072]{1,0:T(8,128)} async-done(((f32[512,3072]{1,0:T(8,128)}), f32[512,3072]{1,0:T(8,128)}) %all-reduce.5.cloned.1.call-update) | async-done | bytes 6291472 | tf_op jit(solution)/shard_map/psum | solution.py:51
  166.8 3.6 %multiply_convert_fusion = bf16[512,3072]{1,0:T(8,128)(2,1)S(1)} fusion(f32[512,3072]{1,0:T(8,128)} %all-reduce.5.cloned.1.call-done), kind=kLoop, calls=%fused_computation.7 | loop fusion | flops 7864320 | bytes 9437184 | tf_op jit(solution)/shard_map/convert_element_type | solution.py:52
  170.4 1.7 copy-done.1
  172.1 4.0 %fusion.8 = bf16[3072,384]{1,0:T(8,128)(2,1)} fusion(bf16[1,3072,384]{2,1,0:T(8,128)(2,1)S(1)} %copy-done.3, bf16[512,3072]{1,0:T(8,128)(2,1)S(1)} %multiply_convert_fusion, bf16[1,512,384]{2,1,0:T(8,128)(2,1)S(1)} %all-gather), kind=kOutput, calls=%fused_computation.12 | convolution fusion | flops 1215037440 | bytes 8257536 | tf_op jit(solution)/shard_map/dot_general | solution.py:71
  176.1 99.6 %all-reduce.7.cloned.1.call-done = bf16[512,3072]{1,0:T(8,128)(2,1)} async-done(((bf16[512,3072]{1,0:T(8,128)(2,1)}), bf16[512,3072]{1,0:T(8,128)(2,1)}) %all-reduce.7.cloned.1.call-update) | async-done | bytes 3145744 | tf_op jit(solution)/shard_map/psum | solution.py:59
  275.7 8.4 %fusion.11 = bf16[384,3072]{0,1:T(8,128)(2,1)} fusion(bf16[1,384,3072]{1,2,0:T(8,128)(2,1)} %copy.9, bf16[512,384]{1,0:T(8,128)(2,1)S(1)} %bitcast.37, f32[512,3072]{1,0:T(8,128)} %all-reduce.5.cloned.1.call-done, bf16[512,3072]{1,0:T(8,128)(2,1)} %all-reduce.7.cloned.1.call-done), kind=kOutput, calls=%fused_computation.16 | convolution fusion | flops 1232338944 | bytes 14548992 | tf_op jit(solution)/shard_map/dot_general | solution.py:67
  284.1 3.7 %fusion.21 = f32[512,384]{1,0:T(8,128)S(1)} fusion(bf16[512,3072]{1,0:T(8,128)(2,1)} %copy-done.1, bf16[3072,384]{1,0:T(8,128)(2,1)S(1)} %copy-done), kind=kOutput, calls=%fused_computation.27 | convolution fusion | flops 1207959552 | bytes 6291456 | tf_op jit(solution)/shard_map/dot_general | solution.py:55
  287.8 27.9 %all_to_all.11 = f32[8,64,384]{2,1,0:T(8,128)S(1)} all-to-all(f32[8,64,384]{2,1,0:T(8,128)S(1)} %bitcast.38), channel_id=1, replica_groups=mesh['row'=16,'col'=8,'rep'=2] {'col'}, dimensions={0} | all-to-all | bytes 1572864 | tf_op jit(solution)/shard_map/all_to_all | solution.py:33
  315.7 0.7 reduce_sum.9
  316.4 7.7 %all-reduce.9.cloned.1.call-done = (bf16[384,3072]{0,1:T(8,128)(2,1)}, bf16[3072,384]{1,0:T(8,128)(2,1)}) async-done(((bf16[384,3072]{0,1:T(8,128)(2,1)}, bf16[3072,384]{1,0:T(8,128)(2,1)}), (bf16[384,3072]{0,1:T(8,128)(2,1)}, bf16[3072,384]{1,0:T(8,128)(2,1)})) %all-reduce.9.cloned.1.call-update) | async-done | bytes 4718608 | tf_op jit(solution)/shard_map/psum | solution.py:83
  324.1 4.3 %copy.10 = bf16[384,3072]{1,0:T(8,128)(2,1)} copy(bf16[384,3072]{0,1:T(8,128)(2,1)} %get-tuple-element.6) | data formatting | bytes 4718592
  328.4 3.3 copy.15
  (7 shorter events, 0.0 us)
Async XLA Ops:
  7.2 50.8 %copy-start = (bf16[3072,384]{1,0:T(8,128)(2,1)S(1)}, bf16[3072,384]{1,0:T(8,128)(2,1)}, u32[]{:S(2)}) copy-start(bf16[3072,384]{1,0:T(8,128)(2,1)} %param.9) | copy-start | bytes 7077892
  7.2 159.7 %all-reduce.5.cloned.1.call-start = ((), (), s32[]{:S(2)}) async-start(), calls=%async_computation.2 | async-start | bytes 12582912 | tf_op jit(solution)/shard_map/psum | solution.py:51
  36.7 0.8 copy-start.2
  36.7 239.0 %all-reduce.7.cloned.1.call-start = ((), (), s32[]{:S(2)}) async-start(), calls=%async_computation.3 | async-start | bytes 6291456 | tf_op jit(solution)/shard_map/psum | solution.py:59
  61.5 262.7 %all-reduce.9.cloned.1.call-start = ((), (), s32[]{:S(2)}) async-start(), calls=%async_computation.4 | async-start | bytes 9437184 | tf_op jit(solution)/shard_map/psum | solution.py:83
  166.8 5.3 %copy-start.3 = (bf16[1,3072,384]{2,1,0:T(8,128)(2,1)S(1)}, bf16[1,3072,384]{2,1,0:T(8,128)(2,1)}, u32[]{:S(2)}) copy-start(bf16[1,3072,384]{2,1,0:T(8,128)(2,1)} %param.11) | copy-start | bytes 7077892
  170.4 1.7 copy-start.1
Sparse Core Ops, SparseCore 0:
  36.9 129.9 all-reduce.4
  170.2 105.4 all-reduce.6
  284.2 39.8 all-reduce.8
where the time goes:
time: 339 us; the launch traced here: 338 us
  waiting for transfers between devices  208 us (61%)
  blocking collectives  70.8 us (21%)
  matrix products  25.6 us (8%)
  local copies, waits for them, and re-layouts  15.3 us (5%)
  between operations  13.8 us (4%)
  other arithmetic  4.23 us (1%)
    psum x1, waiting for transfers between devices, shards(): lax.psum(jnp.dot(inputs, w_in, preferred_element_type=jnp.float32), 'row')  101 us
    psum x1, waiting for transfers between devices, shards(): lax.psum(lax.dot_general(block, w_out, (((1,), (1,)), ((), ())), preferre...  99.6 us
    all_to_all x1, blocking collectives, sum_at_owner(): lax.all_to_all(blocks, axis, split_axis=0, concat_axis=0, tiled=True)  27.9 us
    all_to_all x1, blocking collectives, sent_to_all(): return lax.all_to_all(copies, axis, split_axis=0, concat_axis=0, tiled=True)  22.4 us
    all_gather x1, blocking collectives, shards(): grads = lax.all_gather(cotangent[0], 'col', axis=0, tiled=True)  20.5 us
    unnamed x11, local copies, waits for them, and re-layouts  14.3 us
    dot_general x1, matrix products, shards(): lax.dot_general(inputs, slope, (((0,), (0,)), ((), ())), preferred_elemen...  8.39 us
    psum x1, waiting for transfers between devices, shards(): lax.psum(vote_first, 'rep').astype(jnp.float32)  7.74 us
  transfers between devices with their start and end apart: 3, of which 3 were waited for; matrix products, arithmetic and copies ran while one was open for 6% of the time, Pallas kernels for 0%

commit v1 on v0

--- a/solution.py
+++ b/solution.py
@@ -6,6 +6,28 @@
 
 momentum_decay = 0.9
 vote_scale = 0.3
+
+
+def in_order(pieces, dim):
+    pieces = jnp.moveaxis(pieces, 0, dim)
+    lengths = pieces.shape
+    return pieces.reshape(*lengths[:dim], lengths[dim] * lengths[dim + 1], *lengths[dim + 2 :])
+
+
+def ring_gather(shard, axis, dim):
+    count = lax.axis_size(axis)
+    pairs = [(i, (i + 1) % count) for i in range(count)]
+    back = [(b, a) for a, b in pairs]
+    lower, upper = ([], [])
+    for step in range(count - 1):
+        if step % 2 == 0:
+            lower.append(lax.ppermute(lower[-1] if lower else shard, axis, pairs))
+        else:
+            upper.append(lax.ppermute(upper[-1] if upper else shard, axis, back))
+    pieces = jnp.stack([*lower[::-1], shard, *upper])
+    shift = lax.axis_index(axis) - len(lower)
+    pieces = pieces[(jnp.arange(count) - shift) % count]
+    return in_order(pieces, dim)
 
 
 def joined_along(blocks, dim):
@@ -54,7 +76,7 @@
     mixed = sum_at_owner(
         jnp.dot(block, w_out, preferred_element_type=jnp.float32), "col", 0
     ).astype(jnp.bfloat16)
-    grads = lax.all_gather(cotangent[0], "col", axis=0, tiled=True)
+    grads = ring_gather(cotangent[0], "col", 0)
     block = grads
     back_whole = lax.psum(
         lax.dot_general(

time: 339 us -> 339 us (level)
  blocking collectives: 70.8 us -> 50.3 us
  waiting for transfers between devices: 208 us -> 219 us
  starting transfers between devices: 0.12 us -> 9.01 us
    all_gather x1 -> x0, blocking collectives: 20.5 us -> none  [shards(): grads = lax.all_gather(cotangent[0], 'col', axis=0, tiled=True)]
    ppermute x0 -> x7, waiting for transfers between devices: none -> 8.96 us  [the longest x4 8.95 us: ring_gather(): lower.append(lax.ppermute(lower[-1] if lower else shard, axis, pairs))]
    ppermute x0 -> x7, starting transfers between devices: none -> 8.71 us  [the longest x3 8.36 us: ring_gather(): upper.append(lax.ppermute(upper[-1] if upper else shard, axis, back))]
    unnamed x11 -> x18, local copies, waits for them, and re-layouts: 14.3 us -> 14.4 us
  transfers between devices with their start and end apart: 3 -> 10, of which waited for: 3 -> 7; matrix products, arithmetic and copies ran while one was open for 6% -> 6% of each run, Pallas kernels for 0% -> 0%
where the time goes in v1:
time: 339 us; the launch traced here: 338 us
  waiting for transfers between devices  219 us (65%)
  blocking collectives  50.3 us (15%)
  matrix products  25.6 us (8%)
  local copies, waits for them, and re-layouts  16.1 us (5%)
  between operations  13.9 us (4%)
  starting transfers between devices  9.01 us (3%)
  other arithmetic  4.25 us (1%)
    psum x1, waiting for transfers between devices, shards(): lax.psum(jnp.dot(inputs, w_in, preferred_element_type=jnp.float32), 'row')  103 us
    psum x1, waiting for transfers between devices, shards(): lax.psum(lax.dot_general(block, w_out, (((1,), (1,)), ((), ())), preferre...  99.6 us
    all_to_all x1, blocking collectives, sum_at_owner(): lax.all_to_all(blocks, axis, split_axis=0, concat_axis=0, tiled=True)  27.9 us
    all_to_all x1, blocking collectives, sent_to_all(): return lax.all_to_all(copies, axis, split_axis=0, concat_axis=0, tiled=True)  22.4 us
    unnamed x18, local copies, waits for them, and re-layouts  14.4 us
    ppermute x4, waiting for transfers between devices, ring_gather(): lower.append(lax.ppermute(lower[-1] if lower else shard, axis, pairs))  8.95 us
    dot_general x1, matrix products, shards(): lax.dot_general(inputs, slope, (((0,), (0,)), ((), ())), preferred_elemen...  8.39 us
    ppermute x3, starting transfers between devices, ring_gather(): upper.append(lax.ppermute(upper[-1] if upper else shard, axis, back))  8.36 us
  transfers between devices with their start and end apart: 10, of which 7 were waited for; matrix products, arithmetic and copies ran while one was open for 6% of the time, Pallas kernels for 0%

profile of v1, /device:TPU:1, one launch (start us, length us, event | category | flops | bytes accessed | tf_op | source)
XLA Modules:
  0.0 338.3 jit_solution(12596646234505062026)
XLA Ops:
  7.2 1.0 broadcast_in_dim.2
  8.2 22.4 %all_to_all.10 = bf16[8,64,384]{2,1,0:T(8,128)(2,1)S(1)} all-to-all(bf16[8,64,384]{2,1,0:T(8,128)(2,1)S(1)} %broadcast_in_dim.2), channel_id=1, replica_groups=mesh['row'=16,'col'=8,'rep'=2] {'col'}, dimensions={0} | all-to-all | bytes 786432 | tf_op jit(solution)/shard_map/all_to_all | solution.py:41
  30.6 6.1 %fusion.20 = f32[512,3072]{1,0:T(8,128)} fusion(bf16[512,384]{1,0:T(8,128)(2,1)S(1)} %bitcast.51, bf16[384,3072]{1,0:T(8,128)(2,1)} %param.8), kind=kOutput, calls=%fused_computation.40 | convolution fusion | flops 1207959552 | bytes 9043968 | tf_op jit(solution)/shard_map/dot_general | solution.py:73
  36.8 0.7 copy-done.2
  37.9 3.8 %collective-permute-done = bf16[64,384]{1,0:T(8,128)(2,1)S(1)} collective-permute-done((bf16[64,384]{1,0:T(8,128)(2,1)S(1)}, bf16[64,384]{1,0:T(8,128)(2,1)S(1)}, u32[]{:S(2)}, u32[]{:S(2)}) %collective-permute-start) | collective-permute-done | bytes 49184 | tf_op jit(solution)/shard_map/ppermute | solution.py:24
  41.7 2.7 collective-permute-start.4
  44.3 1.5 collective-permute-done.1
  45.8 2.7 collective-permute-start.5
  48.6 1.8 collective-permute-done.2
  50.4 2.9 collective-permute-start.6
  53.4 1.9 collective-permute-done.3
  56.0 3.5 %convolution_convert_fusion = bf16[512,3072]{1,0:T(8,128)(2,1)} fusion(bf16[512,384]{1,0:T(8,128)(2,1)S(1)} %bitcast.54, bf16[3072,384]{1,0:T(8,128)(2,1)S(1)} %copy-done), kind=kOutput, calls=%fused_computation.18 | convolution fusion | flops 1209532416 | bytes 5898240 | tf_op jit(solution)/shard_map/dot_general | solution.py:82
  59.8 4.3 %copy.9 = bf16[1,384,3072]{1,2,0:T(8,128)(2,1)} copy(bf16[1,384,3072]{2,1,0:T(8,128)(2,1)} %param.10) | data formatting | bytes 4718592 | tf_op args[4]
  64.1 102.8 %all-reduce.5.cloned.1.call-done = f32[512,3072]{1,0:T(8,128)} async-done(((f32[512,3072]{1,0:T(8,128)}), f32[512,3072]{1,0:T(8,128)}) %all-reduce.5.cloned.1.call-update) | async-done | bytes 6291472 | tf_op jit(solution)/shard_map/psum | solution.py:73
  166.9 3.6 %multiply_convert_fusion = bf16[512,3072]{1,0:T(8,128)(2,1)S(1)} fusion(f32[512,3072]{1,0:T(8,128)} %all-reduce.5.cloned.1.call-done), kind=kLoop, calls=%fused_computation.8 | loop fusion | flops 7864320 | bytes 9437184 | tf_op jit(solution)/shard_map/convert_element_type | solution.py:74
  170.5 1.7 copy-done.1
  172.2 4.0 %fusion.8 = bf16[3072,384]{1,0:T(8,128)(2,1)} fusion(bf16[1,3072,384]{2,1,0:T(8,128)(2,1)S(1)} %copy-done.3, bf16[512,3072]{1,0:T(8,128)(2,1)S(1)} %multiply_convert_fusion, bf16[512,384]{1,0:T(8,128)(2,1)S(1)} %bitcast.55), kind=kOutput, calls=%fused_computation.13 | convolution fusion | flops 1215037440 | bytes 8257536 | tf_op jit(solution)/shard_map/dot_general | solution.py:93
  176.1 99.6 %all-reduce.7.cloned.1.call-done = bf16[512,3072]{1,0:T(8,128)(2,1)} async-done(((bf16[512,3072]{1,0:T(8,128)(2,1)}), bf16[512,3072]{1,0:T(8,128)(2,1)}) %all-reduce.7.cloned.1.call-update) | async-done | bytes 3145744 | tf_op jit(solution)/shard_map/psum | solution.py:81
  275.7 8.4 %fusion.11 = bf16[384,3072]{0,1:T(8,128)(2,1)} fusion(bf16[1,384,3072]{1,2,0:T(8,128)(2,1)} %copy.9, bf16[512,384]{1,0:T(8,128)(2,1)S(1)} %bitcast.52, f32[512,3072]{1,0:T(8,128)} %all-reduce.5.cloned.1.call-done, bf16[512,3072]{1,0:T(8,128)(2,1)} %all-reduce.7.cloned.1.call-done), kind=kOutput, calls=%fused_computation.17 | convolution fusion | flops 1232338944 | bytes 14548992 | tf_op jit(solution)/shard_map/dot_general | solution.py:89
  284.2 3.7 %fusion.21 = f32[512,384]{1,0:T(8,128)S(1)} fusion(bf16[512,3072]{1,0:T(8,128)(2,1)} %copy-done.1, bf16[3072,384]{1,0:T(8,128)(2,1)S(1)} %copy-done), kind=kOutput, calls=%fused_computation.41 | convolution fusion | flops 1207959552 | bytes 6291456 | tf_op jit(solution)/shard_map/dot_general | solution.py:77
  287.8 27.9 %all_to_all.11 = f32[8,64,384]{2,1,0:T(8,128)S(1)} all-to-all(f32[8,64,384]{2,1,0:T(8,128)S(1)} %bitcast.53), channel_id=1, replica_groups=mesh['row'=16,'col'=8,'rep'=2] {'col'}, dimensions={0} | all-to-all | bytes 1572864 | tf_op jit(solution)/shard_map/all_to_all | solution.py:55
  316.4 7.7 %all-reduce.9.cloned.1.call-done = (bf16[384,3072]{0,1:T(8,128)(2,1)}, bf16[3072,384]{1,0:T(8,128)(2,1)}) async-done(((bf16[384,3072]{0,1:T(8,128)(2,1)}, bf16[3072,384]{1,0:T(8,128)(2,1)}), (bf16[384,3072]{0,1:T(8,128)(2,1)}, bf16[3072,384]{1,0:T(8,128)(2,1)})) %all-reduce.9.cloned.1.call-update) | async-done | bytes 4718608 | tf_op jit(solution)/shard_map/psum | solution.py:105
  324.2 4.3 %copy.10 = bf16[384,3072]{1,0:T(8,128)(2,1)} copy(bf16[384,3072]{0,1:T(8,128)(2,1)} %get-tuple-element.6) | data formatting | bytes 4718592
  328.4 3.3 copy.22
  (31 shorter events, 2.1 us)
Async XLA Ops:
  7.2 48.8 %copy-start = (bf16[3072,384]{1,0:T(8,128)(2,1)S(1)}, bf16[3072,384]{1,0:T(8,128)(2,1)}, u32[]{:S(2)}) copy-start(bf16[3072,384]{1,0:T(8,128)(2,1)} %param.9) | copy-start | bytes 7077892
  7.2 159.7 %all-reduce.5.cloned.1.call-start = ((), (), s32[]{:S(2)}) async-start(), calls=%async_computation.2 | async-start | bytes 12582912 | tf_op jit(solution)/shard_map/psum | solution.py:73
  36.7 0.8 copy-start.2
  36.7 239.0 %all-reduce.7.cloned.1.call-start = ((), (), s32[]{:S(2)}) async-start(), calls=%async_computation.3 | async-start | bytes 6291456 | tf_op jit(solution)/shard_map/psum | solution.py:81
  37.5 4.2 %collective-permute-start = (bf16[64,384]{1,0:T(8,128)(2,1)S(1)}, bf16[64,384]{1,0:T(8,128)(2,1)S(1)}, u32[]{:S(2)}, u32[]{:S(2)}) collective-permute-start(bf16[64,384]{1,0:T(8,128)(2,1)S(1)} %bitcast.58), channel_id=1, source_target_pairs={{0,2},{2,4},{4,6},{6,8},{8,10},{10,12},{12,14},{14,0},{1,3},{3,5},... | collective-permute-start | bytes 147464 | tf_op jit(solution)/shard_map/ppermute | solution.py:24
  41.7 4.2 %collective-permute-start.1 = (bf16[64,384]{1,0:T(8,128)(2,1)S(1)}, bf16[64,384]{1,0:T(8,128)(2,1)S(1)}, u32[]{:S(2)}, u32[]{:S(2)}) collective-permute-start(bf16[64,384]{1,0:T(8,128)(2,1)S(1)} %collective-permute-done), channel_id=1, source_target_pairs={{0,2},{2,4},{4,6},{6,8},{8,10},{10,12},{12,14},{14,0},{1,3},{3,5},... | collective-permute-start | bytes 147464 | tf_op jit(solution)/shard_map/ppermute | solution.py:24
  41.7 4.2 %collective-permute-start.4 = (bf16[64,384]{1,0:T(8,128)(2,1)S(1)}, bf16[64,384]{1,0:T(8,128)(2,1)S(1)}, u32[]{:S(2)}, u32[]{:S(2)}) collective-permute-start(bf16[64,384]{1,0:T(8,128)(2,1)S(1)} %bitcast.59), channel_id=1, source_target_pairs={{2,0},{4,2},{6,4},{8,6},{10,8},{12,10},{14,12},{0,14},{3,1},{5,3},... | collective-permute-start | bytes 147464 | tf_op jit(solution)/shard_map/ppermute | solution.py:26
  45.8 4.6 %collective-permute-start.2 = (bf16[64,384]{1,0:T(8,128)(2,1)S(1)}, bf16[64,384]{1,0:T(8,128)(2,1)S(1)}, u32[]{:S(2)}, u32[]{:S(2)}) collective-permute-start(bf16[64,384]{1,0:T(8,128)(2,1)S(1)} %collective-permute-done.1), channel_id=1, source_target_pairs={{0,2},{2,4},{4,6},{6,8},{8,10},{10,12},{12,14},{14,0},{1,3},{3,5},... | collective-permute-start | bytes 147464 | tf_op jit(solution)/shard_map/ppermute | solution.py:24
  45.8 4.6 %collective-permute-start.5 = (bf16[64,384]{1,0:T(8,128)(2,1)S(1)}, bf16[64,384]{1,0:T(8,128)(2,1)S(1)}, u32[]{:S(2)}, u32[]{:S(2)}) collective-permute-start(bf16[64,384]{1,0:T(8,128)(2,1)S(1)} %collective-permute-done.4), channel_id=1, source_target_pairs={{2,0},{4,2},{6,4},{8,6},{10,8},{12,10},{14,12},{0,14},{3,1},{5,3},... | collective-permute-start | bytes 147464 | tf_op jit(solution)/shard_map/ppermute | solution.py:26
  50.4 4.8 %collective-permute-start.3 = (bf16[64,384]{1,0:T(8,128)(2,1)S(1)}, bf16[64,384]{1,0:T(8,128)(2,1)S(1)}, u32[]{:S(2)}, u32[]{:S(2)}) collective-permute-start(bf16[64,384]{1,0:T(8,128)(2,1)S(1)} %collective-permute-done.2), channel_id=1, source_target_pairs={{0,2},{2,4},{4,6},{6,8},{8,10},{10,12},{12,14},{14,0},{1,3},{3,5},... | collective-permute-start | bytes 147464 | tf_op jit(solution)/shard_map/ppermute | solution.py:24
  50.4 4.9 %collective-permute-start.6 = (bf16[64,384]{1,0:T(8,128)(2,1)S(1)}, bf16[64,384]{1,0:T(8,128)(2,1)S(1)}, u32[]{:S(2)}, u32[]{:S(2)}) collective-permute-start(bf16[64,384]{1,0:T(8,128)(2,1)S(1)} %collective-permute-done.5), channel_id=1, source_target_pairs={{2,0},{4,2},{6,4},{8,6},{10,8},{12,10},{14,12},{0,14},{3,1},{5,3},... | collective-permute-start | bytes 147464 | tf_op jit(solution)/shard_map/ppermute | solution.py:26
  59.5 264.6 %all-reduce.9.cloned.1.call-start = ((), (), s32[]{:S(2)}) async-start(), calls=%async_computation.4 | async-start | bytes 9437184 | tf_op jit(solution)/shard_map/psum | solution.py:105
  166.9 5.3 %copy-start.3 = (bf16[1,3072,384]{2,1,0:T(8,128)(2,1)S(1)}, bf16[1,3072,384]{2,1,0:T(8,128)(2,1)}, u32[]{:S(2)}) copy-start(bf16[1,3072,384]{2,1,0:T(8,128)(2,1)} %param.11) | copy-start | bytes 7077892
  170.5 1.7 copy-start.1
Sparse Core Ops, SparseCore 0:
  36.9 129.9 all-reduce.4
  170.2 105.4 all-reduce.6
  284.3 39.8 all-reduce.8
